TPU v7x, 32 devices: a whole 2x2x4 slice. The times are simulated.
32 devices in a mesh: batch: 4 (over x, core), seq: 8 (over z, y).
Axes of the slice: x: 2, y: 2, z: 4, core: 2. Of those that a mesh axis runs over, the one named last changes fastest.
Arguments:
- signal: bfloat16 [4, 2048, 256], P('batch', 'seq'), may hold values from -0.3125 to 0.3125
- grad_out: bfloat16 [4, 2048, 256], P('batch', 'seq'), may hold values from -6 to 6
- filter_taps: float32 [2048, 256], P('seq'), may hold values from -0.3125 to 0.3125
- skip_gain: float32 [256], replicated, may hold values from 0.5 to 2
Outputs:
- input_grad: bfloat16 [4, 2048, 256], P('batch', 'seq')
- filter_grad: float32 [2048, 256], P('seq')
All inputs are finite; a program needn't handle non-finite values.
Results may differ from a plain program's by a relative error of at most 0.001.
Values sent between devices are 32-bit elements; how exact they have to be, the bound alone decides.
A program may use at most 64 MiB of HBM per device.

v0:
```python
import jax
import jax.numpy as jnp
from jax import lax
from jax.sharding import PartitionSpec as P


def angle_table(height, width, period):
    product = lax.broadcasted_iota(jnp.int32, (height, width), 0) * lax.broadcasted_iota(
        jnp.int32, (height, width), 1
    )
    return 2.0 * jnp.pi / period * (product % period).astype(jnp.float32)


def angle_of(product, period):
    return 2.0 * jnp.pi / period * (product % period).astype(jnp.float32)


def coarse_order(slot, seq_count):
    pair_index = slot // 2
    odd_slot = slot % 2
    return jnp.where(
        pair_index == 0,
        odd_slot * seq_count,
        jnp.where(odd_slot == 0, pair_index, 2 * seq_count - pair_index),
    )


def contract(form, table, operand):
    return jnp.einsum(form, table, operand, precision=lax.Precision.HIGHEST)


def forward_spectra(columns):
    seq_count = lax.axis_size("seq")
    row_count = columns.shape[0]
    part_rows = row_count // seq_count
    period_len = 2 * row_count * seq_count
    spread = lax.all_to_all(
        columns.reshape(1, row_count, columns.shape[1]),
        "seq",
        split_axis=1,
        concat_axis=0,
        tiled=True,
    )
    slot_grid = lax.broadcasted_iota(jnp.int32, (2 * seq_count, seq_count), 0)
    source_grid = lax.broadcasted_iota(jnp.int32, (2 * seq_count, seq_count), 1)
    first_table = angle_of(coarse_order(slot_grid, seq_count) * source_grid, 2 * seq_count)
    cos_first = jnp.cos(first_table)
    sin_first = jnp.sin(first_table)
    half_width = spread.shape[2] // 2
    real_in = spread[:, :, :half_width]
    imag_in = spread[:, :, half_width:]
    real_part = contract("ks,srw->krw", cos_first, real_in) + contract(
        "ks,srw->krw", sin_first, imag_in
    )
    imag_part = contract("ks,srw->krw", cos_first, imag_in) - contract(
        "ks,srw->krw", sin_first, real_in
    )
    global_row = lax.axis_index("seq") * part_rows + lax.broadcasted_iota(
        jnp.int32, (2 * seq_count, part_rows), 1
    )
    coarse = coarse_order(lax.broadcasted_iota(jnp.int32, (2 * seq_count, part_rows), 0), seq_count)
    phases = angle_of(global_row * coarse, period_len)
    cos_turn = jnp.cos(phases)[:, :, None]
    sin_turn = jnp.sin(phases)[:, :, None]
    rotated = jnp.stack(
        [real_part * cos_turn + imag_part * sin_turn, imag_part * cos_turn - real_part * sin_turn]
    )
    inner_table = angle_table(row_count, row_count, row_count)
    cos_inner = jnp.cos(inner_table)
    sin_inner = jnp.sin(inner_table)
    pieces = lax.all_to_all(rotated, "seq", split_axis=1, concat_axis=2, tiled=True)
    real_sum = contract("qr,krw->kqw", cos_inner, pieces[0]) + contract(
        "qr,krw->kqw", sin_inner, pieces[1]
    )
    imag_sum = contract("qr,krw->kqw", cos_inner, pieces[1]) - contract(
        "qr,krw->kqw", sin_inner, pieces[0]
    )
    return jnp.stack([real_sum, imag_sum])


def split_pairs(packed):
    reversed_q = packed[:, :, ::-1]
    zero_row = jnp.roll(reversed_q[:, 0], 1, axis=1)
    own_pair = jnp.stack([zero_row, reversed_q[:, 1]], axis=1)
    partner = jnp.where(lax.axis_index("seq") == 0, own_pair, reversed_q[:, ::-1])
    first = jnp.stack([0.5 * (packed[0] + partner[0]), 0.5 * (packed[1] - partner[1])])
    second = jnp.stack([0.5 * (packed[1] + partner[1]), 0.5 * (partner[0] - packed[0])])
    return (first, second)


def inverse_rows(spectra):
    seq_count = lax.axis_size("seq")
    row_count = spectra.shape[2]
    period_len = 2 * row_count * seq_count
    inner_table = angle_table(row_count, row_count, row_count)
    cos_inner = jnp.cos(inner_table)
    sin_inner = jnp.sin(inner_table)
    real_sum = contract("qr,krw->kqw", cos_inner, spectra[0]) - contract(
        "qr,krw->kqw", sin_inner, spectra[1]
    )
    imag_sum = contract("qr,krw->kqw", cos_inner, spectra[1]) + contract(
        "qr,krw->kqw", sin_inner, spectra[0]
    )
    coarse = coarse_order(
        2 * lax.axis_index("seq") + lax.broadcasted_iota(jnp.int32, (2, row_count), 0), seq_count
    )
    position = lax.broadcasted_iota(jnp.int32, (2, row_count), 1)
    phases = angle_of(position * coarse, period_len)
    cos_turn = jnp.cos(phases)[:, :, None]
    sin_turn = jnp.sin(phases)[:, :, None]
    rotated = jnp.stack(
        [real_sum * cos_turn - imag_sum * sin_turn, real_sum * sin_turn + imag_sum * cos_turn]
    )
    target_grid = lax.broadcasted_iota(jnp.int32, (seq_count, 2 * seq_count), 0)
    slot_grid = lax.broadcasted_iota(jnp.int32, (seq_count, 2 * seq_count), 1)
    last_table = angle_of(target_grid * coarse_order(slot_grid, seq_count), 2 * seq_count)
    cos_last = jnp.cos(last_table)
    sin_last = jnp.sin(last_table)
    pieces = lax.all_to_all(rotated, "seq", split_axis=2, concat_axis=1, tiled=True)
    value = contract("sk,krw->srw", cos_last, pieces[0]) - contract(
        "sk,krw->srw", sin_last, pieces[1]
    )
    other = contract("sk,krw->srw", sin_last, pieces[0]) + contract(
        "sk,krw->srw", cos_last, pieces[1]
    )
    gathered = (value / period_len, other / period_len)
    gathered = jnp.concatenate([gathered[0], gathered[1]], axis=2)
    home_rows = lax.all_to_all(gathered, "seq", split_axis=0, concat_axis=1, tiled=True)
    return home_rows.reshape(row_count, home_rows.shape[2])


def invert_all(spectra):
    half_width = spectra.shape[3] // 2
    joined = jnp.stack(
        [
            spectra[0, :, :, :half_width] - spectra[1, :, :, half_width:],
            spectra[1, :, :, :half_width] + spectra[0, :, :, half_width:],
        ]
    )
    return inverse_rows(joined)


def shards(signal, grad_out, filter_taps, skip_gain):
    channels = filter_taps.shape[1]
    signal_rows = signal[0].astype(jnp.float32)
    grad_rows = grad_out[0].astype(jnp.float32)
    tap_half = filter_taps.shape[1] // 2
    columns = jnp.concatenate(
        [signal_rows, filter_taps[:, :tap_half], grad_rows, filter_taps[:, tap_half:]], axis=1
    )
    first, second = split_pairs(forward_spectra(columns))
    signal_spec = first[:, :, :, :channels]
    grad_spec = second[:, :, :, :channels]
    own_spec = jnp.concatenate([first[:, :, :, channels:], second[:, :, :, channels:]], axis=3)
    input_spec = jnp.stack(
        [
            grad_spec[0] * own_spec[0] + grad_spec[1] * own_spec[1],
            grad_spec[1] * own_spec[0] - grad_spec[0] * own_spec[1],
        ]
    )
    filter_terms = jnp.stack(
        [
            grad_spec[0] * signal_spec[0] + grad_spec[1] * signal_spec[1],
            grad_spec[1] * signal_spec[0] - grad_spec[0] * signal_spec[1],
        ]
    )
    summed = lax.psum(filter_terms, "batch")
    rows_back = invert_all(jnp.concatenate([input_spec, summed], axis=3))
    filter_grad = rows_back[:, channels:]
    input_grad = (rows_back[:, :channels] + skip_gain[None, :] * grad_rows).astype(jnp.bfloat16)
    return (input_grad[None], filter_grad)


def solution(mesh):
    return jax.shard_map(
        shards,
        mesh=mesh,
        in_specs=(P("batch", "seq", None), P("batch", "seq", None), P("seq", None), P()),
        out_specs=(P("batch", "seq", None), P("seq", None)),
        check_vma=False,
    )
```

profile of v0, /device:TPU:0, one launch (start us, length us, event | category | flops | bytes accessed | tf_op | source)
XLA Modules:
  0.0 231.8 jit_solution(8577959397815715858)
XLA Ops:
  7.2 1.0 fusion.173
  8.2 1.0 bitcast_convert_fusion
  9.2 1.7 copy.37
  10.9 7.3 %all-to-all-start = ((f32[1,256,768]{2,0,1:T(1,128)}), f32[1,256,768]{2,0,1:T(1,128)S(1)}, u32[]{:S(2)}, u32[]{:S(2)}) async-start(f32[1,256,768]{2,0,1:T(1,128)} %copy.37), calls=%async_computation | async-start | bytes 1572864 | tf_op jit(solution)/shard_map/all_to_all | solution.py:37
  18.4 20.0 %all-to-all-done = f32[1,256,768]{2,0,1:T(1,128)S(1)} async-done(((f32[1,256,768]{2,0,1:T(1,128)}), f32[1,256,768]{2,0,1:T(1,128)S(1)}, u32[]{:S(2)}, u32[]{:S(2)}) %all-to-all-start) | async-done | bytes 786464 | tf_op jit(solution)/shard_map/all_to_all | solution.py:37
  38.5 1.0 fusion.16
  39.5 1.0 fusion.20
  40.5 1.0 convolution_subtract_fusion.1
  41.4 1.1 add_bitcast_fusion
  42.7 1.7 copy.40
  44.4 3.6 %all-to-all-start.1 = ((f32[2,16,32,384]{3,2,0,1:T(8,128)}), f32[2,16,32,384]{3,2,0,1:T(8,128)S(1)}, u32[]{:S(2)}, u32[]{:S(2)}) async-start(f32[2,16,32,384]{3,2,0,1:T(8,128)} %copy.40), calls=%async_computation.1 | async-start | bytes 3145728 | tf_op jit(solution)/shard_map/all_to_all | solution.py:71
  48.2 36.9 %all-to-all-done.1 = f32[2,16,32,384]{3,2,0,1:T(8,128)S(1)} async-done(((f32[2,16,32,384]{3,2,0,1:T(8,128)}), f32[2,16,32,384]{3,2,0,1:T(8,128)S(1)}, u32[]{:S(2)}, u32[]{:S(2)}) %all-to-all-start.1) | async-done | bytes 1572896 | tf_op jit(solution)/shard_map/all_to_all | solution.py:71
  85.5 2.2 fusion.36
  87.7 2.2 fusion.34
  89.9 2.2 convolution_subtract_fusion
  92.1 2.2 convolution_add_fusion
  94.3 1.3 pad_maximum_fusion
  95.6 1.3 fusion.4
  96.9 11.2 %rev.4 = f32[2,2,256,384]{2,3,1,0:T(8,128)S(1)} reverse(f32[2,2,256,384]{2,3,1,0:T(8,128)} %pad_maximum_fusion), dimensions={1,2} | reverse | bytes 3145728 | tf_op jit(solution)/shard_map/rev | solution.py:85
  108.1 7.2 %slice.127 = f32[2,1,256,384]{2,3,1,0:T(8,128)} reverse(f32[2,1,256,384]{2,3,1,0:T(8,128)} %get-tuple-element.17), dimensions={2} | reverse | bytes 1572864 | tf_op jit(solution)/shard_map/slice | solution.py:84
  115.3 7.2 %slice.123 = f32[2,1,256,384]{2,3,0,1:T(8,128)} reverse(f32[2,1,256,384]{2,3,0,1:T(8,128)} %get-tuple-element.16), dimensions={2} | reverse | bytes 1572864 | tf_op jit(solution)/shard_map/slice | solution.py:83
  122.5 1.2 slice.150
  123.8 1.4 maximum_bitcast_fusion.1
  125.4 0.4 fusion.13
  125.9 0.7 copy-done
  126.7 0.2 copy-done.2
  126.9 1.0 pad_maximum_fusion.3
  128.4 0.2 copy-done.3
  128.6 1.1 fusion.2
  129.7 33.8 %all-reduce.2.cloned.1.call-done = f32[2,2,256,256]{2,3,1,0:T(8,128)} async-done(((f32[2,2,256,256]{2,3,1,0:T(8,128)}), f32[2,2,256,256]{2,3,1,0:T(8,128)}) %all-reduce.2.cloned.1.call-update) | async-done | bytes 1048592 | tf_op jit(solution)/shard_map/psum | solution.py:167
  163.5 1.7 fusion.15
  165.2 1.6 fusion.30
  166.7 1.6 fusion.32
  168.3 1.6 convolution_add_fusion.2
  169.9 1.6 subtract_bitcast_fusion.1
  171.6 0.6 copy.49
  172.2 30.5 %all_to_all.51 = f32[2,2,256,256]{3,1,0,2:T(2,128)S(1)} all-to-all(f32[2,2,256,256]{3,1,0,2:T(2,128)S(1)} %copy.49), channel_id=1, replica_groups=mesh['batch'=4,'seq'=8] {'seq'}, dimensions={2} | all-to-all | bytes 2097152 | tf_op jit(solution)/shard_map/all_to_all | solution.py:119
  203.1 0.4 copy.51
  203.5 0.4 squeeze.19
  203.9 0.4 fusion.69
  204.3 0.4 fusion.77
  204.7 0.4 copy.52
  205.1 0.4 squeeze.20
  205.5 0.4 fusion
  205.9 0.4 fusion.1
  206.4 0.3 copy.53
  206.7 17.4 %all_to_all.52 = f32[8,32,512]{2,1,0:T(8,128)S(1)} all-to-all(f32[8,32,512]{2,1,0:T(8,128)S(1)} %copy.53), channel_id=1, replica_groups=mesh['batch'=4,'seq'=8] {'seq'}, dimensions={0} | all-to-all | bytes 1048576 | tf_op jit(solution)/shard_map/all_to_all | solution.py:128
  224.2 0.8 fusion.172
  (37 shorter events, 2.3 us)
Async XLA Ops:
  10.9 27.5 %all-to-all-start = ((f32[1,256,768]{2,0,1:T(1,128)}), f32[1,256,768]{2,0,1:T(1,128)S(1)}, u32[]{:S(2)}, u32[]{:S(2)}) async-start(f32[1,256,768]{2,0,1:T(1,128)} %copy.37), calls=%async_computation | async-start | bytes 1572864 | tf_op jit(solution)/shard_map/all_to_all | solution.py:37
  44.4 40.8 %all-to-all-start.1 = ((f32[2,16,32,384]{3,2,0,1:T(8,128)}), f32[2,16,32,384]{3,2,0,1:T(8,128)S(1)}, u32[]{:S(2)}, u32[]{:S(2)}) async-start(f32[2,16,32,384]{3,2,0,1:T(8,128)} %copy.40), calls=%async_computation.1 | async-start | bytes 3145728 | tf_op jit(solution)/shard_map/all_to_all | solution.py:71
  48.0 115.5 %all-reduce.2.cloned.1.call-start = ((), (), s32[]{:S(2)}) async-start(), calls=%async_computation.4 | async-start | bytes 2097152 | tf_op jit(solution)/shard_map/psum | solution.py:167
  122.5 2.6 %copy-start.4 = (f32[2,1,256,384]{2,3,1,0:T(8,128)S(1)}, f32[2,1,256,384]{2,3,1,0:T(8,128)}, u32[]{:S(2)}) copy-start(f32[2,1,256,384]{2,3,1,0:T(8,128)} %slice.127) | copy-start | bytes 2359300
  125.8 0.9 copy-start
  125.8 1.1 copy-start.2
  126.9 1.5 copy-start.1
  126.9 1.7 copy-start.3
  206.3 17.8 %copy-start.5 = (bf16[1,256,256]{2,1,0:T(8,128)(2,1)S(1)}, bf16[1,256,256]{2,1,0:T(8,128)(2,1)}, u32[]{:S(2)}) copy-start(bf16[1,256,256]{2,1,0:T(8,128)(2,1)} %param.5) | copy-start | bytes 393220
  206.4 17.8 %copy-start.6 = (f32[256]{0:T(256)S(1)}, f32[256]{0:T(256)}, u32[]{:S(2)}) copy-start(f32[256]{0:T(256)} %param.7) | copy-start | bytes 3076
Sparse Core Ops, SparseCore 0:
  128.1 35.3 all-reduce.1
where the time goes:
time: 234 us; the launch traced here: 232 us
  waiting for transfers between devices  90.7 us (39%)
  blocking collectives  48 us (21%)
  local copies, waits for them, and re-layouts  36 us (15%)
  matrix products  20.8 us (9%)
  between operations  14.4 us (6%)
  starting transfers between devices  11.1 us (5%)
  other arithmetic  10.9 us (5%)
    all_to_all x1, waiting for transfers between devices, forward_spectra(): lax.all_to_all(rotated, 'seq', split_axis=1, concat_axis=2, tiled=True)  36.9 us
    psum x1, waiting for transfers between devices, shards(): summed = lax.psum(filter_terms, 'batch')  33.8 us
    all_to_all x1, blocking collectives, inverse_rows(): lax.all_to_all(rotated, 'seq', split_axis=2, concat_axis=1, tiled=True)  30.5 us
    dot_general x16, matrix products, contract(): return jnp.einsum(form, table, operand, precision=lax.Precision.HIGHEST)  20.8 us
    all_to_all x1, waiting for transfers between devices, forward_spectra(): lax.all_to_all(columns.reshape(1, row_count, columns.shape[1]), 'seq', sp...  20 us
    all_to_all x1, blocking collectives, inverse_rows(): lax.all_to_all(gathered, 'seq', split_axis=0, concat_axis=1, tiled=True)  17.4 us
    rev x1, local copies, waits for them, and re-layouts, split_pairs(): reversed_q[:, ::-1]  11.2 us
    slice x2, local copies, waits for them, and re-layouts, split_pairs(): zero_row = jnp.roll(reversed_q[:, 0], 1, axis=1)  8.44 us
  transfers between devices with their start and end apart: 3, of which 3 were waited for; matrix products, arithmetic and copies ran while one was open for 1% of the time, Pallas kernels for 0%

commit v1 on v0

--- a/solution.py
+++ b/solution.py
@@ -1,7 +1,334 @@
+import functools
+import math
+
 import jax
 import jax.numpy as jnp
+import numpy as np
 from jax import lax
+from jax.experimental import pallas as pl
+from jax.experimental.pallas import tpu as pltpu
 from jax.sharding import PartitionSpec as P
+
+MESH = pl.DeviceIdType.MESH
+F32 = jnp.float32
+BF16 = jnp.bfloat16
+GRAD, TAPS, SIGNAL, INPUT, FILTER = range(5)
+
+
+def weighted(terms):
+    total = None
+    for factor, array in terms:
+        if array is None or abs(factor) < 1e-12:
+            continue
+        if total is None:
+            if abs(factor - 1.0) < 1e-12:
+                total = array
+            else:
+                total = array * factor
+        elif abs(factor - 1.0) < 1e-12:
+            total = total + array
+        elif abs(factor + 1.0) < 1e-12:
+            total = total - array
+        else:
+            total = total + array * factor
+    return total
+
+
+def added(left, right):
+    return weighted([(1.0, left), (1.0, right)])
+
+
+def subtracted(left, right):
+    return weighted([(1.0, left), (-1.0, right)])
+
+
+def turn(real, imag, cos_turn, sin_turn):
+    if imag is None:
+        return real * cos_turn, -(real * sin_turn)
+    return real * cos_turn + imag * sin_turn, imag * cos_turn - real * sin_turn
+
+
+def coarse_forward(blocks):
+    count = len(blocks)
+    result = [None] * (count + 1)
+    for k in range(count // 2 + 1):
+        sums = []
+        for parity in (0, 1):
+            angles = [(math.pi * ((s * k) % (2 * count)) / count, s) for s in range(parity, count, 2)]
+            sums.append(
+                (
+                    weighted([(math.cos(a), blocks[s]) for a, s in angles]),
+                    weighted([(-math.sin(a), blocks[s]) for a, s in angles]),
+                )
+            )
+        (even_re, even_im), (odd_re, odd_im) = sums
+        result[k] = (added(even_re, odd_re), added(even_im, odd_im))
+        if k != count - k:
+            result[count - k] = (subtracted(even_re, odd_re), subtracted(odd_im, even_im))
+    return result
+
+
+def coarse_inverse(terms, scale):
+    count = len(terms) - 1
+    pairs = []
+    for k in range(count // 2 + 1):
+        weight = scale if k == 0 else 2.0 * scale
+        real, imag = terms[k]
+        if k == count - k:
+            pairs.append((weight, real, imag, real, imag))
+        else:
+            other_re, other_im = terms[count - k]
+            pairs.append((weight, real + other_re, imag - other_im, real - other_re, imag + other_im))
+    blocks = []
+    for s in range(count):
+        parts = []
+        for k, (weight, even_re, even_im, odd_re, odd_im) in enumerate(pairs):
+            angle = math.pi * ((s * k) % (2 * count)) / count
+            parts.append((weight * math.cos(angle) * (1 if abs(math.cos(angle)) > 1e-9 else 0), odd_re if s % 2 else even_re))
+            parts.append((weight * math.sin(angle) * (1 if abs(math.sin(angle)) > 1e-9 else 0), odd_im if s % 2 else even_im))
+        blocks.append(weighted(parts))
+    return blocks
+
+
+def fused_kernel(
+    groups, seqs,
+    signal_ref, grad_ref, tap_ref, skip_ref, high_ref, low_ref, cos_ref, sin_ref,
+    input_ref, filter_ref,
+    grad_out_buf, signal_out_buf, tap_out_buf, grad_in, signal_in, tap_in,
+    input_out, filter_out, input_in, filter_in,
+    grad_rows, grad_spec, signal_rows, signal_spec, input_rows, filter_rows, filter_spec,
+    send_sems, recv_sems,
+):
+    count = groups * seqs
+    coarse = seqs + 1
+    own, rows = grad_in.shape[1:]
+    channels = count * own
+    group, seq = lax.axis_index("batch"), lax.axis_index("seq")
+    me = group * seqs + seq
+    scale = 1.0 / (2 * seqs * rows)
+    re, im = pl.ds(0, rows), pl.ds(rows, rows)
+
+    def peer(step):
+        place = lax.rem(me + step, count)
+        return place, lax.div(place, seqs), lax.rem(place, seqs)
+
+    barrier = pltpu.get_barrier_semaphore()
+
+    def greet(step, carry):
+        _, to_group, to_seq = peer(step)
+        pl.semaphore_signal(
+            barrier, inc=1, device_id={"batch": to_group, "seq": to_seq}, device_id_type=MESH
+        )
+        return carry
+
+    lax.fori_loop(1, count, greet, 0)
+
+    def transfer(source, target, kind, to_group, to_seq):
+        return pltpu.make_async_remote_copy(
+            src_ref=source,
+            dst_ref=target,
+            send_sem=send_sems.at[kind],
+            recv_sem=recv_sems.at[kind],
+            device_id={"batch": to_group, "seq": to_seq},
+            device_id_type=MESH,
+        )
+
+    def all_of(buffer, blocks, kind):
+        _, to_group, to_seq = peer(1)
+        view = buffer.at[pl.ds(0, blocks)]
+        return transfer(view, view, kind, to_group, to_seq)
+
+    grad_out_buf[...] = grad_ref[...].astype(F32).T.reshape(count, own, rows)
+    tap_out_buf[...] = tap_ref[...].T.reshape(count, own, rows)
+    signal_out_buf[...] = signal_ref[...].astype(F32).T.reshape(count, own, rows)
+    pl.semaphore_wait(barrier, count - 1)
+
+    def send_taps(step, carry):
+        to_seq = lax.rem(seq + step, seqs)
+        place = group * seqs + to_seq
+        transfer(tap_out_buf.at[place], tap_in.at[seq], TAPS, group, to_seq).start()
+        return carry
+
+    def send_grads(step, carry):
+        place, to_group, to_seq = peer(step)
+        transfer(grad_out_buf.at[place], grad_in.at[me], GRAD, to_group, to_seq).start()
+        return carry
+
+    def send_signals(step, carry):
+        place, to_group, to_seq = peer(step)
+        transfer(signal_out_buf.at[place], signal_in.at[me], SIGNAL, to_group, to_seq).start()
+        return carry
+
+    lax.fori_loop(1, seqs, send_taps, 0)
+    lax.fori_loop(1, count, send_grads, 0)
+    lax.fori_loop(1, count, send_signals, 0)
+    grad_in[me] = grad_out_buf[me]
+    tap_in[seq] = tap_out_buf[me]
+    signal_in[me] = signal_out_buf[me]
+
+    def spread(blocks, target, first_row):
+        place = pl.ds(first_row, own)
+        for k, (real, imag) in enumerate(coarse_forward(blocks)):
+            real, imag = turn(real, imag, cos_ref[k], sin_ref[k])
+            target[k, place, re] = real
+            target[k, place, im] = imag
+
+    def fine(source, target):
+        lines = source.shape[0] * source.shape[1]
+        value = source[...].reshape(lines, 2 * rows)
+        high = value.astype(BF16)
+        low = (value - high.astype(F32)).astype(BF16)
+        product = functools.partial(jnp.dot, preferred_element_type=F32)
+        total = product(high, high_ref[...]) + product(low, high_ref[...]) + product(high, low_ref[...])
+        target[...] = total.reshape(target.shape)
+
+    def collect(source, first_row):
+        place = pl.ds(first_row, own)
+        terms = [
+            turn(source[k, place, re], source[k, place, im], cos_ref[k], sin_ref[k])
+            for k in range(coarse)
+        ]
+        return coarse_inverse(terms, scale)
+
+    def row_of(index):
+        return pl.multiple_of(index * own, own)
+
+    all_of(tap_in, seqs - 1, TAPS).wait_recv()
+    spread([tap_in[s] for s in range(seqs)], grad_rows, groups * own)
+    all_of(grad_in, count - 1, GRAD).wait_recv()
+
+    def spread_grad(index, carry):
+        spread([grad_in[index * seqs + s] for s in range(seqs)], grad_rows, row_of(index))
+        return carry
+
+    lax.fori_loop(0, groups, spread_grad, 0)
+    fine(grad_rows, grad_spec)
+
+    def multiply_taps(index, carry):
+        place, fixed = pl.ds(row_of(index), own), pl.ds(groups * own, own)
+        for k in range(coarse):
+            grad_re, grad_im = grad_spec[k, place, re], grad_spec[k, place, im]
+            tap_re, tap_im = grad_spec[k, fixed, re], grad_spec[k, fixed, im]
+            input_rows[k, place, re] = grad_re * tap_re + grad_im * tap_im
+            input_rows[k, place, im] = grad_re * tap_im - grad_im * tap_re
+        return carry
+
+    lax.fori_loop(0, groups, multiply_taps, 0)
+    fine(input_rows, input_rows)
+
+    def collect_input(index, carry):
+        for s, block in enumerate(collect(input_rows, row_of(index))):
+            input_out[index * seqs + s] = block
+        return carry
+
+    lax.fori_loop(0, groups, collect_input, 0)
+
+    def send_inputs(step, carry):
+        place, to_group, to_seq = peer(step)
+        transfer(input_out.at[place], input_in.at[me], INPUT, to_group, to_seq).start()
+        return carry
+
+    lax.fori_loop(1, count, send_inputs, 0)
+    input_in[me] = input_out[me]
+
+    all_of(signal_in, count - 1, SIGNAL).wait_recv()
+
+    def spread_signal(index, carry):
+        spread([signal_in[index * seqs + s] for s in range(seqs)], signal_rows, row_of(index))
+        return carry
+
+    lax.fori_loop(0, groups, spread_signal, 0)
+    fine(signal_rows, signal_spec)
+    for k in range(coarse):
+        real, imag = None, None
+        for index in range(groups):
+            place = pl.ds(index * own, own)
+            grad_re, grad_im = grad_spec[k, place, re], grad_spec[k, place, im]
+            signal_re, signal_im = signal_spec[k, place, re], signal_spec[k, place, im]
+            real = added(real, grad_re * signal_re + grad_im * signal_im)
+            imag = added(imag, grad_re * signal_im - grad_im * signal_re)
+        filter_rows[k, :, re] = real
+        filter_rows[k, :, im] = imag
+    fine(filter_rows, filter_spec)
+    for s, block in enumerate(collect(filter_spec, 0)):
+        filter_out[s] = block
+
+    def send_filters(step, carry):
+        _, to_group, to_seq = peer(step)
+        transfer(filter_out.at[to_seq], filter_in.at[me], FILTER, to_group, to_seq).start()
+        return carry
+
+    lax.fori_loop(1, count, send_filters, 0)
+    filter_in[me] = filter_out[seq]
+
+    all_of(input_in, count - 1, INPUT).wait_recv()
+    gradient = input_in[...].reshape(channels, rows).T + skip_ref[...] * grad_ref[...].astype(F32)
+    input_ref[...] = gradient.astype(BF16)
+    all_of(filter_in, count - 1, FILTER).wait_recv()
+    filter_ref[...] = filter_in[...].reshape(channels, rows).T
+    for kind, buffer in ((GRAD, grad_in), (SIGNAL, signal_in), (INPUT, input_in), (FILTER, filter_in)):
+        all_of(buffer, count - 1, kind).wait_send()
+    all_of(tap_in, seqs - 1, TAPS).wait_send()
+
+
+def fine_tables(rows):
+    grid = np.arange(rows)
+    angle = 2.0 * np.pi / rows * (np.outer(grid, grid) % rows)
+    table = np.block([[np.cos(angle), -np.sin(angle)], [np.sin(angle), np.cos(angle)]]).astype(np.float32)
+    high = table.astype(BF16)
+    return high, (table - high.astype(np.float32)).astype(BF16)
+
+
+def turn_tables(seqs, rows, lines):
+    angle = np.pi / (seqs * rows) * np.outer(np.arange(seqs + 1), np.arange(rows))
+    wide = np.broadcast_to(angle[:, None, :], (seqs + 1, lines, rows))
+    return np.cos(wide).astype(np.float32), np.sin(wide).astype(np.float32)
+
+
+def fused_shards(groups, seqs, signal, grad_out, filter_taps, skip_gain):
+    rows, channels = filter_taps.shape
+    count, coarse = groups * seqs, seqs + 1
+    own = channels // count
+    high, low = fine_tables(rows)
+    cos_turn, sin_turn = turn_tables(seqs, rows, own)
+    blocks = pltpu.VMEM((count, own, rows), F32)
+    few = pltpu.VMEM((seqs, own, rows), F32)
+    lines = lambda number: pltpu.VMEM((coarse, number * own, 2 * rows), F32)
+    vmem = pl.BlockSpec(memory_space=pltpu.VMEM)
+    input_grad, filter_grad = pl.pallas_call(
+        functools.partial(fused_kernel, groups, seqs),
+        out_shape=(
+            jax.ShapeDtypeStruct((rows, channels), BF16),
+            jax.ShapeDtypeStruct((rows, channels), F32),
+        ),
+        in_specs=[vmem] * 8,
+        out_specs=(vmem, vmem),
+        scratch_shapes=[
+            blocks, blocks, blocks, blocks, blocks, few,
+            blocks, few, blocks, blocks,
+            lines(groups + 1), lines(groups + 1), lines(groups), lines(groups),
+            lines(groups), lines(1), lines(1),
+            pltpu.SemaphoreType.DMA((5,)),
+            pltpu.SemaphoreType.DMA((5,)),
+        ],
+        compiler_params=pltpu.CompilerParams(
+            collective_id=0, has_side_effects=True, vmem_limit_bytes=48 * 1024 * 1024
+        ),
+    )(
+        signal[0], grad_out[0], filter_taps, skip_gain[None, :],
+        jnp.asarray(high), jnp.asarray(low), jnp.asarray(cos_turn), jnp.asarray(sin_turn),
+    )
+    return input_grad[None], filter_grad
+
+
+def fits_fused(groups, seqs, signal, filter_taps):
+    rows, channels = filter_taps.shape
+    return (
+        signal.shape[0] == 1
+        and seqs % 2 == 0
+        and rows % 128 == 0
+        and channels % (8 * groups * seqs) == 0
+    )
 
 
 def angle_table(height, width, period):
@@ -172,8 +499,15 @@
 
 
 def solution(mesh):
+    groups, seqs = mesh.shape["batch"], mesh.shape["seq"]
+
+    def either(signal, grad_out, filter_taps, skip_gain):
+        if fits_fused(groups, seqs, signal, filter_taps):
+            return fused_shards(groups, seqs, signal, grad_out, filter_taps, skip_gain)
+        return shards(signal, grad_out, filter_taps, skip_gain)
+
     return jax.shard_map(
-        shards,
+        either,
         mesh=mesh,
         in_specs=(P("batch", "seq", None), P("batch", "seq", None), P("seq", None), P()),
         out_specs=(P("batch", "seq", None), P("seq", None)),

time: 234 us -> 42.3 us (0.18)
  waiting for transfers between devices: 90.7 us -> 0 us
  blocking collectives: 48 us -> 0 us
  Pallas kernels: 0 us -> 32.7 us
  local copies, waits for them, and re-layouts: 36 us -> 8.64 us
  matrix products: 20.8 us -> 0 us
  between operations: 14.4 us -> 0.65 us
  starting transfers between devices: 11.1 us -> 0 us
  other arithmetic: 10.9 us -> 0 us
    all_to_all x2 -> x0, waiting for transfers between devices: 56.9 us -> none  [the longest x1 36.9 us: forward_spectra(): lax.all_to_all(rotated, 'seq', split_axis=1, concat_axis=2, tiled=True)]
    all_to_all x2 -> x0, blocking collectives: 48 us -> none  [the longest x1 30.5 us: inverse_rows(): lax.all_to_all(rotated, 'seq', split_axis=2, concat_axis=1, tiled=True)]
    psum x1 -> x0, waiting for transfers between devices: 33.8 us -> none  [shards(): summed = lax.psum(filter_terms, 'batch')]
    pallas_call x0 -> x1, Pallas kernels: none -> 32.7 us  [fused_shards(): pl.pallas_call(functools.partial(fused_kernel, groups, seqs), out_shape=(...]
    dot_general x16 -> x0, matrix products: 20.8 us -> none  [contract(): return jnp.einsum(form, table, operand, precision=lax.Precision.HIGHEST)]
    slice x11 -> x0, local copies, waits for them, and re-layouts: 17.8 us -> none  [the longest x2 8.44 us: split_pairs(): zero_row = jnp.roll(reversed_q[:, 0], 1, axis=1)]
    rev x1 -> x0, local copies, waits for them, and re-layouts: 11.2 us -> none  [split_pairs(): reversed_q[:, ::-1]]
    all_to_all x2 -> x0, starting transfers between devices: 10.9 us -> none  [the longest x1 7.31 us: forward_spectra(): lax.all_to_all(columns.reshape(1, row_count, columns.shape[1]), 'seq', sp...]
  transfers between devices with their start and end apart: 3 -> 0, of which waited for: 3 -> 0; matrix products, arithmetic and copies ran while one was open for 1% -> 0% of each run, Pallas kernels for 0% -> 0%
where the time goes in v1:
time: 42.3 us; the launch traced here: 42 us
  Pallas kernels  32.7 us (77%)
  local copies, waits for them, and re-layouts  8.64 us (20%)
  between operations  0.65 us (2%)
    pallas_call x1, Pallas kernels, fused_shards(): pl.pallas_call(functools.partial(fused_kernel, groups, seqs), out_shape=(...  32.7 us
    unnamed x18, local copies, waits for them, and re-layouts  8.64 us

profile of v1, /device:TPU:0, one launch (start us, length us, event | category | flops | bytes accessed | tf_op | source)
XLA Modules:
  0.0 42.0 jit_solution(8292161028424872435)
XLA Ops:
  0.6 0.0 copy-start.7
  0.6 0.7 %copy-done.7 = f32[256]{0:T(256)S(1)} copy-done((f32[256]{0:T(256)S(1)}, f32[256]{0:T(256)}, u32[]{:S(2)}) %copy-start.7) | copy-done | bytes 1048
  1.3 0.0 copy-start
  1.3 1.0 %copy-done = bf16[512,512]{1,0:T(8,128)(2,1)S(1)} copy-done((bf16[512,512]{1,0:T(8,128)(2,1)S(1)}, bf16[512,512]{1,0:T(8,128)(2,1)}, u32[]{:S(2)}) %copy-start) | copy-done | bytes 524312
  2.4 0.0 copy-start.1
  2.4 1.0 %copy-done.1 = bf16[512,512]{1,0:T(8,128)(2,1)S(1)} copy-done((bf16[512,512]{1,0:T(8,128)(2,1)S(1)}, bf16[512,512]{1,0:T(8,128)(2,1)}, u32[]{:S(2)}) %copy-start.1) | copy-done | bytes 524312
  3.4 0.0 copy-start.2
  3.4 0.9 %copy-done.2 = f32[256,256]{1,0:T(8,128)S(1)} copy-done((f32[256,256]{1,0:T(8,128)S(1)}, f32[256,256]{1,0:T(8,128)}, u32[]{:S(2)}) %copy-start.2) | copy-done | bytes 262168
  4.3 0.0 copy-start.3
  4.3 0.9 %copy-done.3 = bf16[1,256,256]{2,1,0:T(8,128)(2,1)S(1)} copy-done((bf16[1,256,256]{2,1,0:T(8,128)(2,1)S(1)}, bf16[1,256,256]{2,1,0:T(8,128)(2,1)}, u32[]{:S(2)}) %copy-start.3) | copy-done | bytes 131096
  5.2 0.0 copy-start.4
  5.3 0.9 %copy-done.4 = bf16[1,256,256]{2,1,0:T(8,128)(2,1)S(1)} copy-done((bf16[1,256,256]{2,1,0:T(8,128)(2,1)S(1)}, bf16[1,256,256]{2,1,0:T(8,128)(2,1)}, u32[]{:S(2)}) %copy-start.4) | copy-done | bytes 131096
  6.2 0.0 copy-start.5
  6.2 0.9 %copy-done.5 = f32[9,8,256]{2,1,0:T(8,128)S(1)} copy-done((f32[9,8,256]{2,1,0:T(8,128)S(1)}, f32[9,8,256]{2,1,0:T(8,128)}, u32[]{:S(2)}) %copy-start.5) | copy-done | bytes 73752
  7.0 0.0 copy-start.6
  7.0 0.9 %copy-done.6 = f32[9,8,256]{2,1,0:T(8,128)S(1)} copy-done((f32[9,8,256]{2,1,0:T(8,128)S(1)}, f32[9,8,256]{2,1,0:T(8,128)}, u32[]{:S(2)}) %copy-start.6) | copy-done | bytes 73752
  7.9 32.7 %shard_map.95 = (bf16[256,256]{1,0:T(8,128)(2,1)S(1)}, f32[256,256]{1,0:T(8,128)S(1)}) custom-call(bf16[256,256]{1,0:T(8,128)(2,1)S(1)} %bitcast.4, bf16[256,256]{1,0:T(8,128)(2,1)S(1)} %bitcast.5, f32[256,256]{1,0:T(8,128)S(1)} %copy-done.2, f32[1,256]{1,0:T(1,128)S(1)} %bitcast.7, bf16[512,512]{1,0:T(8,128)(2,1)S(1)} %copy-done.1, ...), custom_call_target="tpu_custom_call" | custom-call | tf_op jit(solution)/shard_map/pallas_call | solution.py:298
  40.6 0.7 %copy.12 = bf16[1,256,256]{2,1,0:T(8,128)(2,1)} copy(bf16[1,256,256]{2,1,0:T(8,128)(2,1)S(1)} %bitcast.6) | data formatting | bytes 262144
  41.3 0.7 %copy.13 = f32[256,256]{1,0:T(8,128)} copy(f32[256,256]{1,0:T(8,128)S(1)} %get-tuple-element.9) | data formatting | bytes 524288
Async XLA Ops:
  0.6 0.7 %copy-start.7 = (f32[256]{0:T(256)S(1)}, f32[256]{0:T(256)}, u32[]{:S(2)}) copy-start(f32[256]{0:T(256)} %param.11) | copy-start | bytes 3076
  1.3 1.0 %copy-start = (bf16[512,512]{1,0:T(8,128)(2,1)S(1)}, bf16[512,512]{1,0:T(8,128)(2,1)}, u32[]{:S(2)}) copy-start(bf16[512,512]{1,0:T(8,128)(2,1)} %constant.9.clone.low_ref) | copy-start | bytes 1572868
  2.4 1.0 %copy-start.1 = (bf16[512,512]{1,0:T(8,128)(2,1)S(1)}, bf16[512,512]{1,0:T(8,128)(2,1)}, u32[]{:S(2)}) copy-start(bf16[512,512]{1,0:T(8,128)(2,1)} %constant.8.clone.high_ref) | copy-start | bytes 1572868
  3.4 0.9 %copy-start.2 = (f32[256,256]{1,0:T(8,128)S(1)}, f32[256,256]{1,0:T(8,128)}, u32[]{:S(2)}) copy-start(f32[256,256]{1,0:T(8,128)} %tap_ref.1) | copy-start | bytes 786436
  4.3 0.9 %copy-start.3 = (bf16[1,256,256]{2,1,0:T(8,128)(2,1)S(1)}, bf16[1,256,256]{2,1,0:T(8,128)(2,1)}, u32[]{:S(2)}) copy-start(bf16[1,256,256]{2,1,0:T(8,128)(2,1)} %param.8) | copy-start | bytes 393220
  5.2 0.9 %copy-start.4 = (bf16[1,256,256]{2,1,0:T(8,128)(2,1)S(1)}, bf16[1,256,256]{2,1,0:T(8,128)(2,1)}, u32[]{:S(2)}) copy-start(bf16[1,256,256]{2,1,0:T(8,128)(2,1)} %param.9) | copy-start | bytes 393220
  6.2 0.9 %copy-start.5 = (f32[9,8,256]{2,1,0:T(8,128)S(1)}, f32[9,8,256]{2,1,0:T(8,128)}, u32[]{:S(2)}) copy-start(f32[9,8,256]{2,1,0:T(8,128)} %constant.11.clone.sin_ref) | copy-start | bytes 221188
  7.0 0.9 %copy-start.6 = (f32[9,8,256]{2,1,0:T(8,128)S(1)}, f32[9,8,256]{2,1,0:T(8,128)}, u32[]{:S(2)}) copy-start(f32[9,8,256]{2,1,0:T(8,128)} %constant.10.clone.cos_ref) | copy-start | bytes 221188

commit v2 on v1

--- a/solution.py
+++ b/solution.py
@@ -12,7 +12,7 @@
 MESH = pl.DeviceIdType.MESH
 F32 = jnp.float32
 BF16 = jnp.bfloat16
-GRAD, TAPS, SIGNAL, INPUT, FILTER = range(5)
+GRAD, TAPS, SIGNAL, INPUT, FILTER, FORWARD = range(6)
 
 
 def weighted(terms):
@@ -92,12 +92,13 @@
 
 def fused_kernel(
     groups, seqs,
+    signal_hbm, grad_hbm, tap_hbm, skip_hbm, high_hbm, low_hbm, cos_hbm, sin_hbm,
+    input_ref, filter_ref,
     signal_ref, grad_ref, tap_ref, skip_ref, high_ref, low_ref, cos_ref, sin_ref,
-    input_ref, filter_ref,
     grad_out_buf, signal_out_buf, tap_out_buf, grad_in, signal_in, tap_in,
     input_out, filter_out, input_in, filter_in,
     grad_rows, grad_spec, signal_rows, signal_spec, input_rows, filter_rows, filter_spec,
-    send_sems, recv_sems,
+    send_sems, recv_sems, load_sems,
 ):
     count = groups * seqs
     coarse = seqs + 1
@@ -108,9 +109,38 @@
     scale = 1.0 / (2 * seqs * rows)
     re, im = pl.ds(0, rows), pl.ds(rows, rows)
 
+    parity, pair = lax.rem(group, 2), lax.div(group, 2)
+    half_seqs, half_groups = seqs // 2, groups // 2
+    upper, inner = lax.div(seq, half_seqs), lax.rem(seq, half_seqs)
+
+    def load(index, source, target):
+        return pltpu.make_async_copy(source, target, load_sems.at[index])
+
+    loads = [
+        load(index, source, target)
+        for index, (source, target) in enumerate(
+            (
+                (grad_hbm, grad_ref), (tap_hbm, tap_ref), (signal_hbm, signal_ref),
+                (cos_hbm, cos_ref), (sin_hbm, sin_ref), (high_hbm, high_ref),
+                (low_hbm, low_ref), (skip_hbm, skip_ref),
+            )
+        )
+    ]
+    for copy in loads:
+        copy.start()
+
+    def seq_at(step):
+        other = lax.rem(upper + 1 + lax.div(step, half_seqs), 2)
+        return other * half_seqs + lax.rem(inner + step, half_seqs)
+
     def peer(step):
-        place = lax.rem(me + step, count)
-        return place, lax.div(place, seqs), lax.rem(place, seqs)
+        to_seq = seq_at(lax.div(step, groups))
+        to_group = lax.rem(group + step, groups)
+        return to_group * seqs + to_seq, to_group, to_seq
+
+    def over_peers(body, total, own_step):
+        lax.fori_loop(0, own_step, body, 0)
+        lax.fori_loop(own_step + 1, total, body, 0)
 
     barrier = pltpu.get_barrier_semaphore()
 
@@ -121,7 +151,7 @@
         )
         return carry
 
-    lax.fori_loop(1, count, greet, 0)
+    over_peers(greet, count, half_seqs * groups)
 
     def transfer(source, target, kind, to_group, to_seq):
         return pltpu.make_async_remote_copy(
@@ -134,17 +164,18 @@
         )
 
     def all_of(buffer, blocks, kind):
-        _, to_group, to_seq = peer(1)
+        _, to_group, to_seq = peer(0)
         view = buffer.at[pl.ds(0, blocks)]
         return transfer(view, view, kind, to_group, to_seq)
 
+    loads[GRAD].wait()
     grad_out_buf[...] = grad_ref[...].astype(F32).T.reshape(count, own, rows)
+    loads[TAPS].wait()
     tap_out_buf[...] = tap_ref[...].T.reshape(count, own, rows)
-    signal_out_buf[...] = signal_ref[...].astype(F32).T.reshape(count, own, rows)
     pl.semaphore_wait(barrier, count - 1)
 
     def send_taps(step, carry):
-        to_seq = lax.rem(seq + step, seqs)
+        to_seq = seq_at(step)
         place = group * seqs + to_seq
         transfer(tap_out_buf.at[place], tap_in.at[seq], TAPS, group, to_seq).start()
         return carry
@@ -159,9 +190,11 @@
         transfer(signal_out_buf.at[place], signal_in.at[me], SIGNAL, to_group, to_seq).start()
         return carry
 
-    lax.fori_loop(1, seqs, send_taps, 0)
-    lax.fori_loop(1, count, send_grads, 0)
-    lax.fori_loop(1, count, send_signals, 0)
+    over_peers(send_taps, seqs, half_seqs)
+    over_peers(send_grads, count, half_seqs * groups)
+    loads[SIGNAL].wait()
+    signal_out_buf[...] = signal_ref[...].astype(F32).T.reshape(count, own, rows)
+    over_peers(send_signals, count, half_seqs * groups)
     grad_in[me] = grad_out_buf[me]
     tap_in[seq] = tap_out_buf[me]
     signal_in[me] = signal_out_buf[me]
@@ -193,6 +226,8 @@
     def row_of(index):
         return pl.multiple_of(index * own, own)
 
+    for copy in loads[3:]:
+        copy.wait()
     all_of(tap_in, seqs - 1, TAPS).wait_recv()
     spread([tap_in[s] for s in range(seqs)], grad_rows, groups * own)
     all_of(grad_in, count - 1, GRAD).wait_recv()
@@ -228,7 +263,7 @@
         transfer(input_out.at[place], input_in.at[me], INPUT, to_group, to_seq).start()
         return carry
 
-    lax.fori_loop(1, count, send_inputs, 0)
+    over_peers(send_inputs, count, half_seqs * groups)
     input_in[me] = input_out[me]
 
     all_of(signal_in, count - 1, SIGNAL).wait_recv()
@@ -254,20 +289,37 @@
         filter_out[s] = block
 
     def send_filters(step, carry):
-        _, to_group, to_seq = peer(step)
-        transfer(filter_out.at[to_seq], filter_in.at[me], FILTER, to_group, to_seq).start()
-        return carry
-
-    lax.fori_loop(1, count, send_filters, 0)
-    filter_in[me] = filter_out[seq]
-
+        to_seq = seq_at(lax.div(step, half_groups))
+        to_group = 2 * lax.rem(pair + step, half_groups) + parity
+        place = pair * seqs + seq
+        transfer(
+            filter_out.at[to_seq], filter_in.at[parity, place], FILTER, to_group, to_seq
+        ).start()
+        return carry
+
+    over_peers(send_filters, seqs * half_groups, half_seqs * half_groups)
+    filter_in[parity, pair * seqs + seq] = filter_out[seq]
+
+    half = count // 2
     all_of(input_in, count - 1, INPUT).wait_recv()
     gradient = input_in[...].reshape(channels, rows).T + skip_ref[...] * grad_ref[...].astype(F32)
     input_ref[...] = gradient.astype(BF16)
-    all_of(filter_in, count - 1, FILTER).wait_recv()
-    filter_ref[...] = filter_in[...].reshape(channels, rows).T
-    for kind, buffer in ((GRAD, grad_in), (SIGNAL, signal_in), (INPUT, input_in), (FILTER, filter_in)):
+    all_of(filter_in.at[0], half - 1, FILTER).wait_recv()
+    mine = filter_in.at[parity]
+    partner = 2 * pair + 1 - parity
+    forward = transfer(mine, mine, FORWARD, partner, seq)
+    forward.start()
+    forward.wait_recv()
+    parts = [
+        filter_in[which, first * seqs : (first + 1) * seqs].reshape(seqs * own, rows)
+        for first in range(half_groups)
+        for which in range(2)
+    ]
+    filter_ref[...] = jnp.concatenate(parts, axis=0).T
+    for kind, buffer in ((GRAD, grad_in), (SIGNAL, signal_in), (INPUT, input_in)):
         all_of(buffer, count - 1, kind).wait_send()
+    all_of(filter_in.at[0], half - 1, FILTER).wait_send()
+    forward.wait_send()
     all_of(tap_in, seqs - 1, TAPS).wait_send()
 
 
@@ -295,21 +347,28 @@
     few = pltpu.VMEM((seqs, own, rows), F32)
     lines = lambda number: pltpu.VMEM((coarse, number * own, 2 * rows), F32)
     vmem = pl.BlockSpec(memory_space=pltpu.VMEM)
+    hbm = pl.BlockSpec(memory_space=pltpu.HBM)
+    turns = pltpu.VMEM((coarse, own, rows), F32)
+    table = pltpu.VMEM((2 * rows, 2 * rows), BF16)
     input_grad, filter_grad = pl.pallas_call(
         functools.partial(fused_kernel, groups, seqs),
         out_shape=(
             jax.ShapeDtypeStruct((rows, channels), BF16),
             jax.ShapeDtypeStruct((rows, channels), F32),
         ),
-        in_specs=[vmem] * 8,
+        in_specs=[hbm] * 8,
         out_specs=(vmem, vmem),
         scratch_shapes=[
+            pltpu.VMEM((rows, channels), BF16), pltpu.VMEM((rows, channels), BF16),
+            pltpu.VMEM((rows, channels), F32), pltpu.VMEM((1, channels), F32),
+            table, table, turns, turns,
             blocks, blocks, blocks, blocks, blocks, few,
-            blocks, few, blocks, blocks,
+            blocks, few, blocks, pltpu.VMEM((2, count // 2, own, rows), F32),
             lines(groups + 1), lines(groups + 1), lines(groups), lines(groups),
             lines(groups), lines(1), lines(1),
-            pltpu.SemaphoreType.DMA((5,)),
-            pltpu.SemaphoreType.DMA((5,)),
+            pltpu.SemaphoreType.DMA((6,)),
+            pltpu.SemaphoreType.DMA((6,)),
+            pltpu.SemaphoreType.DMA((8,)),
         ],
         compiler_params=pltpu.CompilerParams(
             collective_id=0, has_side_effects=True, vmem_limit_bytes=48 * 1024 * 1024
@@ -326,6 +385,7 @@
     return (
         signal.shape[0] == 1
         and seqs % 2 == 0
+        and groups % 2 == 0
         and rows % 128 == 0
         and channels % (8 * groups * seqs) == 0
     )

time: 42.3 us -> 44 us (1.040)
  Pallas kernels: 32.7 us -> 34.3 us
    pallas_call x1, Pallas kernels: 32.7 us -> 34.3 us  [fused_shards(): pl.pallas_call(functools.partial(fused_kernel, groups, seqs), out_shape=(...]
where the time goes in v2:
time: 44 us; the launch traced here: 43.6 us
  Pallas kernels  34.3 us (78%)
  local copies, waits for them, and re-layouts  8.64 us (20%)
  between operations  0.65 us (1%)
    pallas_call x1, Pallas kernels, fused_shards(): pl.pallas_call(functools.partial(fused_kernel, groups, seqs), out_shape=(...  34.3 us
    unnamed x18, local copies, waits for them, and re-layouts  8.64 us

profile of v2, /device:TPU:0, one launch (start us, length us, event | category | flops | bytes accessed | tf_op | source)
XLA Modules:
  0.0 43.6 jit_solution(649324165280814213)
XLA Ops:
  0.6 0.0 copy-start.7
  0.6 0.7 %copy-done.7 = f32[256]{0:T(256)S(1)} copy-done((f32[256]{0:T(256)S(1)}, f32[256]{0:T(256)}, u32[]{:S(2)}) %copy-start.7) | copy-done | bytes 1048
  1.3 0.0 copy-start
  1.3 1.0 %copy-done = bf16[512,512]{1,0:T(8,128)(2,1)S(1)} copy-done((bf16[512,512]{1,0:T(8,128)(2,1)S(1)}, bf16[512,512]{1,0:T(8,128)(2,1)}, u32[]{:S(2)}) %copy-start) | copy-done | bytes 524312
  2.4 0.0 copy-start.1
  2.4 1.0 %copy-done.1 = bf16[512,512]{1,0:T(8,128)(2,1)S(1)} copy-done((bf16[512,512]{1,0:T(8,128)(2,1)S(1)}, bf16[512,512]{1,0:T(8,128)(2,1)}, u32[]{:S(2)}) %copy-start.1) | copy-done | bytes 524312
  3.4 0.0 copy-start.2
  3.4 0.9 %copy-done.2 = f32[256,256]{1,0:T(8,128)S(1)} copy-done((f32[256,256]{1,0:T(8,128)S(1)}, f32[256,256]{1,0:T(8,128)}, u32[]{:S(2)}) %copy-start.2) | copy-done | bytes 262168
  4.3 0.0 copy-start.3
  4.3 0.9 %copy-done.3 = bf16[1,256,256]{2,1,0:T(8,128)(2,1)S(1)} copy-done((bf16[1,256,256]{2,1,0:T(8,128)(2,1)S(1)}, bf16[1,256,256]{2,1,0:T(8,128)(2,1)}, u32[]{:S(2)}) %copy-start.3) | copy-done | bytes 131096
  5.2 0.0 copy-start.4
  5.3 0.9 %copy-done.4 = bf16[1,256,256]{2,1,0:T(8,128)(2,1)S(1)} copy-done((bf16[1,256,256]{2,1,0:T(8,128)(2,1)S(1)}, bf16[1,256,256]{2,1,0:T(8,128)(2,1)}, u32[]{:S(2)}) %copy-start.4) | copy-done | bytes 131096
  6.2 0.0 copy-start.5
  6.2 0.9 %copy-done.5 = f32[9,8,256]{2,1,0:T(8,128)S(1)} copy-done((f32[9,8,256]{2,1,0:T(8,128)S(1)}, f32[9,8,256]{2,1,0:T(8,128)}, u32[]{:S(2)}) %copy-start.5) | copy-done | bytes 73752
  7.0 0.0 copy-start.6
  7.0 0.9 %copy-done.6 = f32[9,8,256]{2,1,0:T(8,128)S(1)} copy-done((f32[9,8,256]{2,1,0:T(8,128)S(1)}, f32[9,8,256]{2,1,0:T(8,128)}, u32[]{:S(2)}) %copy-start.6) | copy-done | bytes 73752
  7.9 34.3 %shard_map.95 = (bf16[256,256]{1,0:T(8,128)(2,1)S(1)}, f32[256,256]{1,0:T(8,128)S(1)}) custom-call(bf16[256,256]{1,0:T(8,128)(2,1)S(1)} %bitcast.4, bf16[256,256]{1,0:T(8,128)(2,1)S(1)} %bitcast.5, f32[256,256]{1,0:T(8,128)S(1)} %copy-done.2, f32[1,256]{1,0:T(1,128)S(1)} %bitcast.7, bf16[512,512]{1,0:T(8,128)(2,1)S(1)} %copy-done.1, ...), custom_call_target="tpu_custom_call" | custom-call | tf_op jit(solution)/shard_map/pallas_call | solution.py:353
  42.3 0.7 %copy.12 = bf16[1,256,256]{2,1,0:T(8,128)(2,1)} copy(bf16[1,256,256]{2,1,0:T(8,128)(2,1)S(1)} %bitcast.6) | data formatting | bytes 262144
  42.9 0.7 %copy.13 = f32[256,256]{1,0:T(8,128)} copy(f32[256,256]{1,0:T(8,128)S(1)} %get-tuple-element.9) | data formatting | bytes 524288
Async XLA Ops:
  0.6 0.7 %copy-start.7 = (f32[256]{0:T(256)S(1)}, f32[256]{0:T(256)}, u32[]{:S(2)}) copy-start(f32[256]{0:T(256)} %param.11) | copy-start | bytes 3076
  1.3 1.0 %copy-start = (bf16[512,512]{1,0:T(8,128)(2,1)S(1)}, bf16[512,512]{1,0:T(8,128)(2,1)}, u32[]{:S(2)}) copy-start(bf16[512,512]{1,0:T(8,128)(2,1)} %constant.9.clone.low_hbm) | copy-start | bytes 1572868
  2.4 1.0 %copy-start.1 = (bf16[512,512]{1,0:T(8,128)(2,1)S(1)}, bf16[512,512]{1,0:T(8,128)(2,1)}, u32[]{:S(2)}) copy-start(bf16[512,512]{1,0:T(8,128)(2,1)} %constant.8.clone.high_hbm) | copy-start | bytes 1572868
  3.4 0.9 %copy-start.2 = (f32[256,256]{1,0:T(8,128)S(1)}, f32[256,256]{1,0:T(8,128)}, u32[]{:S(2)}) copy-start(f32[256,256]{1,0:T(8,128)} %tap_hbm.1) | copy-start | bytes 786436
  4.3 0.9 %copy-start.3 = (bf16[1,256,256]{2,1,0:T(8,128)(2,1)S(1)}, bf16[1,256,256]{2,1,0:T(8,128)(2,1)}, u32[]{:S(2)}) copy-start(bf16[1,256,256]{2,1,0:T(8,128)(2,1)} %param.8) | copy-start | bytes 393220
  5.2 0.9 %copy-start.4 = (bf16[1,256,256]{2,1,0:T(8,128)(2,1)S(1)}, bf16[1,256,256]{2,1,0:T(8,128)(2,1)}, u32[]{:S(2)}) copy-start(bf16[1,256,256]{2,1,0:T(8,128)(2,1)} %param.9) | copy-start | bytes 393220
  6.2 0.9 %copy-start.5 = (f32[9,8,256]{2,1,0:T(8,128)S(1)}, f32[9,8,256]{2,1,0:T(8,128)}, u32[]{:S(2)}) copy-start(f32[9,8,256]{2,1,0:T(8,128)} %constant.11.clone.sin_hbm) | copy-start | bytes 221188
  7.0 0.9 %copy-start.6 = (f32[9,8,256]{2,1,0:T(8,128)S(1)}, f32[9,8,256]{2,1,0:T(8,128)}, u32[]{:S(2)}) copy-start(f32[9,8,256]{2,1,0:T(8,128)} %constant.10.clone.cos_hbm) | copy-start | bytes 221188

commit v3 on v2

--- a/solution.py
+++ b/solution.py
@@ -371,7 +371,7 @@
             pltpu.SemaphoreType.DMA((8,)),
         ],
         compiler_params=pltpu.CompilerParams(
-            collective_id=0, has_side_effects=True, vmem_limit_bytes=48 * 1024 * 1024
+            collective_id=0, has_side_effects=True, vmem_limit_bytes=67_043_328
         ),
     )(
         signal[0], grad_out[0], filter_taps, skip_gain[None, :],

time: 44 us -> 37.7 us (0.86)
  local copies, waits for them, and re-layouts: 8.64 us -> 2.32 us
    unnamed x18 -> x4, local copies, waits for them, and re-layouts: 8.64 us -> 2.32 us
where the time goes in v3:
time: 37.7 us; the launch traced here: 37.5 us
  Pallas kernels  34.5 us (92%)
  local copies, waits for them, and re-layouts  2.32 us (6%)
  between operations  0.65 us (2%)
    pallas_call x1, Pallas kernels, fused_shards(): pl.pallas_call(functools.partial(fused_kernel, groups, seqs), out_shape=(...  34.5 us
    unnamed x4, local copies, waits for them, and re-layouts  2.32 us

profile of v3, /device:TPU:0, one launch (start us, length us, event | category | flops | bytes accessed | tf_op | source)
XLA Modules:
  0.0 37.5 jit_solution(5577227448916811290)
XLA Ops:
  0.6 34.5 %shard_map.95 = (bf16[256,256]{1,0:T(8,128)(2,1)}, f32[256,256]{1,0:T(8,128)}) custom-call(bf16[256,256]{1,0:T(8,128)(2,1)} %bitcast.4, bf16[256,256]{1,0:T(8,128)(2,1)} %bitcast.5, f32[256,256]{1,0:T(8,128)} %tap_hbm.1, f32[1,256]{1,0:T(1,128)} %bitcast.7, bf16[512,512]{1,0:T(8,128)(2,1)} %constant.8.clone.high_hbm, ...), custom_call_target="tpu_custom_call" | custom-call | tf_op jit(solution)/shard_map/pallas_call | solution.py:353
  35.2 0.0 copy-start
  35.2 1.6 %copy.12 = bf16[1,256,256]{2,1,0:T(8,128)(2,1)} copy(bf16[1,256,256]{2,1,0:T(8,128)(2,1)} %bitcast.6) | data formatting | bytes 262144
  36.8 0.0 copy-done
  36.8 0.7 %copy.13 = f32[256,256]{1,0:T(8,128)} copy(f32[256,256]{1,0:T(8,128)S(1)} %copy-done) | data formatting | bytes 524288
Async XLA Ops:
  35.2 1.6 %copy-start = (f32[256,256]{1,0:T(8,128)S(1)}, f32[256,256]{1,0:T(8,128)}, u32[]{:S(2)}) copy-start(f32[256,256]{1,0:T(8,128)} %get-tuple-element.9) | copy-start | bytes 786436

commit v4 on v3

--- a/solution.py
+++ b/solution.py
@@ -97,7 +97,7 @@
     signal_ref, grad_ref, tap_ref, skip_ref, high_ref, low_ref, cos_ref, sin_ref,
     grad_out_buf, signal_out_buf, tap_out_buf, grad_in, signal_in, tap_in,
     input_out, filter_out, input_in, filter_in,
-    grad_rows, grad_spec, signal_rows, signal_spec, input_rows, filter_rows, filter_spec,
+    tap_rows, tap_spec, grad_rows, grad_spec, signal_rows, signal_spec, input_rows, filter_rows, filter_spec,
     send_sems, recv_sems, load_sems,
 ):
     count = groups * seqs
@@ -229,47 +229,65 @@
     for copy in loads[3:]:
         copy.wait()
     all_of(tap_in, seqs - 1, TAPS).wait_recv()
-    spread([tap_in[s] for s in range(seqs)], grad_rows, groups * own)
+    spread([tap_in[s] for s in range(seqs)], tap_rows, 0)
+    fine(tap_rows, tap_spec)
     all_of(grad_in, count - 1, GRAD).wait_recv()
 
-    def spread_grad(index, carry):
-        spread([grad_in[index * seqs + s] for s in range(seqs)], grad_rows, row_of(index))
-        return carry
-
-    lax.fori_loop(0, groups, spread_grad, 0)
-    fine(grad_rows, grad_spec)
-
-    def multiply_taps(index, carry):
-        place, fixed = pl.ds(row_of(index), own), pl.ds(groups * own, own)
-        for k in range(coarse):
-            grad_re, grad_im = grad_spec[k, place, re], grad_spec[k, place, im]
-            tap_re, tap_im = grad_spec[k, fixed, re], grad_spec[k, fixed, im]
-            input_rows[k, place, re] = grad_re * tap_re + grad_im * tap_im
-            input_rows[k, place, im] = grad_re * tap_im - grad_im * tap_re
-        return carry
-
-    lax.fori_loop(0, groups, multiply_taps, 0)
-    fine(input_rows, input_rows)
-
-    def collect_input(index, carry):
-        for s, block in enumerate(collect(input_rows, row_of(index))):
-            input_out[index * seqs + s] = block
-        return carry
-
-    lax.fori_loop(0, groups, collect_input, 0)
-
-    def send_inputs(step, carry):
-        place, to_group, to_seq = peer(step)
-        transfer(input_out.at[place], input_in.at[me], INPUT, to_group, to_seq).start()
-        return carry
-
-    over_peers(send_inputs, count, half_seqs * groups)
+    def group_at(index):
+        return lax.rem(2 * pair + index, groups)
+
+    def input_part(first):
+        source, spectrum, lines = grad_rows.at[first], grad_spec.at[first], input_rows.at[first]
+
+        def spread_grad(index, carry):
+            here = group_at(2 * first + index)
+            spread([grad_in[here * seqs + s] for s in range(seqs)], source, row_of(index))
+            return carry
+
+        lax.fori_loop(0, 2, spread_grad, 0)
+        fine(source, spectrum)
+
+        def multiply_taps(index, carry):
+            place = pl.ds(row_of(index), own)
+            for k in range(coarse):
+                grad_re, grad_im = spectrum[k, place, re], spectrum[k, place, im]
+                tap_re, tap_im = tap_spec[k, :, re], tap_spec[k, :, im]
+                lines[k, place, re] = grad_re * tap_re + grad_im * tap_im
+                lines[k, place, im] = grad_re * tap_im - grad_im * tap_re
+            return carry
+
+        lax.fori_loop(0, 2, multiply_taps, 0)
+        fine(lines, lines)
+
+        def collect_input(index, carry):
+            here = group_at(2 * first + index)
+            for s, block in enumerate(collect(lines, row_of(index))):
+                input_out[here * seqs + s] = block
+            return carry
+
+        lax.fori_loop(0, 2, collect_input, 0)
+
+        def send_inputs(step, carry):
+            to_seq = seq_at(lax.div(step, 2))
+            to_group = group_at(2 * first + lax.rem(parity + step, 2))
+            place = to_group * seqs + to_seq
+            transfer(input_out.at[place], input_in.at[me], INPUT, to_group, to_seq).start()
+            return carry
+
+        if first == 0:
+            over_peers(send_inputs, 2 * seqs, 2 * half_seqs)
+        else:
+            lax.fori_loop(0, 2 * seqs, send_inputs, 0)
+
+    for first in reversed(range(half_groups)):
+        input_part(first)
     input_in[me] = input_out[me]
 
     all_of(signal_in, count - 1, SIGNAL).wait_recv()
 
     def spread_signal(index, carry):
-        spread([signal_in[index * seqs + s] for s in range(seqs)], signal_rows, row_of(index))
+        here = group_at(index)
+        spread([signal_in[here * seqs + s] for s in range(seqs)], signal_rows, row_of(index))
         return carry
 
     lax.fori_loop(0, groups, spread_signal, 0)
@@ -278,7 +296,8 @@
         real, imag = None, None
         for index in range(groups):
             place = pl.ds(index * own, own)
-            grad_re, grad_im = grad_spec[k, place, re], grad_spec[k, place, im]
+            which, local = index // 2, pl.ds(index % 2 * own, own)
+            grad_re, grad_im = grad_spec[which, k, local, re], grad_spec[which, k, local, im]
             signal_re, signal_im = signal_spec[k, place, re], signal_spec[k, place, im]
             real = added(real, grad_re * signal_re + grad_im * signal_im)
             imag = added(imag, grad_re * signal_im - grad_im * signal_re)
@@ -346,6 +365,7 @@
     blocks = pltpu.VMEM((count, own, rows), F32)
     few = pltpu.VMEM((seqs, own, rows), F32)
     lines = lambda number: pltpu.VMEM((coarse, number * own, 2 * rows), F32)
+    pairs = pltpu.VMEM((groups // 2, coarse, 2 * own, 2 * rows), F32)
     vmem = pl.BlockSpec(memory_space=pltpu.VMEM)
     hbm = pl.BlockSpec(memory_space=pltpu.HBM)
     turns = pltpu.VMEM((coarse, own, rows), F32)
@@ -364,8 +384,8 @@
             table, table, turns, turns,
             blocks, blocks, blocks, blocks, blocks, few,
             blocks, few, blocks, pltpu.VMEM((2, count // 2, own, rows), F32),
-            lines(groups + 1), lines(groups + 1), lines(groups), lines(groups),
-            lines(groups), lines(1), lines(1),
+            lines(1), lines(1), pairs, pairs, lines(groups), lines(groups),
+            pairs, lines(1), lines(1),
             pltpu.SemaphoreType.DMA((6,)),
             pltpu.SemaphoreType.DMA((6,)),
             pltpu.SemaphoreType.DMA((8,)),

time: 37.7 us -> 36.9 us (0.979)
  Pallas kernels: 34.5 us -> 33.7 us
    pallas_call x1, Pallas kernels: 34.5 us -> 33.7 us  [fused_shards(): pl.pallas_call(functools.partial(fused_kernel, groups, seqs), out_shape=(...]
where the time goes in v4:
time: 36.9 us; the launch traced here: 36.7 us
  Pallas kernels  33.7 us (91%)
  local copies, waits for them, and re-layouts  2.32 us (6%)
  between operations  0.65 us (2%)
    pallas_call x1, Pallas kernels, fused_shards(): pl.pallas_call(functools.partial(fused_kernel, groups, seqs), out_shape=(...  33.7 us
    unnamed x4, local copies, waits for them, and re-layouts  2.32 us

profile of v4, /device:TPU:0, one launch (start us, length us, event | category | flops | bytes accessed | tf_op | source)
XLA Modules:
  0.0 36.7 jit_solution(16560641909089088464)
XLA Ops:
  0.6 33.7 %shard_map.95 = (bf16[256,256]{1,0:T(8,128)(2,1)}, f32[256,256]{1,0:T(8,128)}) custom-call(bf16[256,256]{1,0:T(8,128)(2,1)} %bitcast.4, bf16[256,256]{1,0:T(8,128)(2,1)} %bitcast.5, f32[256,256]{1,0:T(8,128)} %tap_hbm.1, f32[1,256]{1,0:T(1,128)} %bitcast.7, bf16[512,512]{1,0:T(8,128)(2,1)} %constant.8.clone.high_hbm, ...), custom_call_target="tpu_custom_call" | custom-call | tf_op jit(solution)/shard_map/pallas_call | solution.py:373
  34.4 0.0 copy-start
  34.4 1.6 %copy.12 = bf16[1,256,256]{2,1,0:T(8,128)(2,1)} copy(bf16[1,256,256]{2,1,0:T(8,128)(2,1)} %bitcast.6) | data formatting | bytes 262144
  36.0 0.0 copy-done
  36.0 0.7 %copy.13 = f32[256,256]{1,0:T(8,128)} copy(f32[256,256]{1,0:T(8,128)S(1)} %copy-done) | data formatting | bytes 524288
Async XLA Ops:
  34.4 1.6 %copy-start = (f32[256,256]{1,0:T(8,128)S(1)}, f32[256,256]{1,0:T(8,128)}, u32[]{:S(2)}) copy-start(f32[256,256]{1,0:T(8,128)} %get-tuple-element.9) | copy-start | bytes 786436
